TPU v7x, 32 devices: a whole 2x2x4 slice. The times are simulated.
32 devices in a mesh: row: 8 (over z, y), col: 4 (over x, core).
Axes of the slice: x: 2, y: 2, z: 4, core: 2. Of those that a mesh axis runs over, the one named last changes fastest.
Arguments:
- moment: bfloat16 [2, 4096, 4096], P(None, 'row', 'col'), may hold values from -6 to 6
- second: float32 [2, 4096, 4096], P(None, 'row', 'col'), may hold values from 0.04 to 2
- left_old: bfloat16 [2, 4096, 4096], P(None, 'col', 'row'), may hold values from -0.09375 to 0.09375
- left_new: bfloat16 [2, 4096, 4096], P(None, 'col', 'row'), may hold values from -0.09375 to 0.09375
- right_old: bfloat16 [4096, 4096], P('row', 'col'), may hold values from -0.09375 to 0.09375
- right_new: bfloat16 [4096, 4096], P('row', 'col'), may hold values from -0.09375 to 0.09375
Outputs:
- moment_new: bfloat16 [2, 4096, 4096], P(None, 'row', 'col')
- direction: bfloat16 [2, 4096, 4096], P(None, 'row', 'col')
All inputs are finite; a program needn't handle non-finite values.
Results may differ from a plain program's by a relative error of at most 0.03.
Values may be sent and summed in bfloat16 or wider, within the bound.
A program may use at most 128 MiB of HBM per device.

v0:
```python
import jax
import jax.numpy as jnp
from jax import lax
from jax.sharding import PartitionSpec as P


def fold_stacked(left_panel, incoming):
    return jnp.einsum("bij,bjk->bik", left_panel, incoming, preferred_element_type=jnp.float32)


def fold_right(right_panel, incoming):
    return jnp.einsum("bik,qk->biq", incoming, right_panel, preferred_element_type=jnp.float32)


def local(moment, second, left_old, left_new, right_old, right_new):
    old_right_rows = lax.all_gather(right_old, "col", axis=1, tiled=True)
    right_terms = jnp.dot(right_new.T, old_right_rows, preferred_element_type=jnp.float32)
    right_panel = lax.psum(right_terms.astype(jnp.bfloat16), "row")
    old_rows = lax.all_gather(left_old, "row", axis=2, tiled=True)
    left_terms = jnp.einsum("bwi,bwj->bij", left_new, old_rows, preferred_element_type=jnp.float32)
    left_panel = lax.psum(left_terms.astype(jnp.bfloat16), "col")
    summed = fold_stacked(left_panel, lax.all_gather(moment, "row", axis=1, tiled=True))
    rotated = summed.astype(jnp.bfloat16)
    result = fold_right(right_panel, lax.all_gather(rotated, "col", axis=2, tiled=True))
    moment_new = result.astype(jnp.bfloat16)
    direction = (moment_new.astype(jnp.float32) / (jnp.sqrt(second) + 1e-08)).astype(jnp.bfloat16)
    return (moment_new, direction)


def solution(mesh):
    return jax.shard_map(
        local,
        mesh=mesh,
        in_specs=(
            P(None, "row", "col"),
            P(None, "row", "col"),
            P(None, "col", "row"),
            P(None, "col", "row"),
            P("row", "col"),
            P("row", "col"),
        ),
        out_specs=(P(None, "row", "col"), P(None, "row", "col")),
        check_vma=False,
    )
```

profile of v0, /device:TPU:0, one launch (start us, length us, event | category | flops | bytes accessed | tf_op | source)
XLA Modules:
  0.0 1013.9 jit_solution(3959504421610417472)
XLA Ops:
  7.2 0.0 copy-start
  7.2 0.0 all-gather.5.cloned.1.call-start
  7.2 0.7 all-gather.5.cloned.1.call-update
  7.9 0.0 all-gather.11.cloned.1.call-start
  8.0 0.7 all-gather.11.cloned.1.call-update
  8.7 0.0 all-gather.7.cloned.1.call-start
  8.7 0.7 all-gather.7.cloned.1.call-update
  9.4 0.0 all-reduce.3.cloned.1.call-start
  9.4 230.6 %all-gather.5.cloned.1.call-done = bf16[2,1024,4096]{2,1,0:T(8,128)(2,1)} async-done(((bf16[2,1024,512]{2,1,0:T(8,128)(2,1)}), bf16[2,1024,4096]{2,1,0:T(8,128)(2,1)}) %all-gather.5.cloned.1.call-update) | async-done | bytes 16777232 | tf_op jit(solution)/shard_map/all_gather | solution.py:19
  240.1 0.0 copy-done
  240.1 17.1 %convolution_convert_fusion.1 = bf16[2,512,4096]{2,1,0:T(8,128)(2,1)} fusion(bf16[2,1024,512]{2,1,0:T(8,128)(2,1)S(1)} %copy-done, bf16[2,1024,4096]{2,1,0:T(8,128)(2,1)} %all-gather.5.cloned.1.call-done), kind=kOutput, calls=%fused_computation.3 | convolution fusion | flops 8594128896 | bytes 27262976 | tf_op jit(solution)/shard_map/bwi,bwj->bij/dot_general | solution.py:20
  257.2 0.0 copy-start.2
  257.2 0.0 all-reduce.3.cloned.1.call-update
  257.2 0.0 all-reduce.5.cloned.1.call-start
  257.2 17.1 %all-gather.11.cloned.1.call-done = bf16[512,4096]{1,0:T(8,128)(2,1)} async-done(((bf16[512,1024]{1,0:T(8,128)(2,1)}), bf16[512,4096]{1,0:T(8,128)(2,1)}) %all-gather.11.cloned.1.call-update) | async-done | bytes 4194320 | tf_op jit(solution)/shard_map/all_gather | solution.py:16
  274.3 0.0 copy-done.2
  274.3 8.9 convolution_convert_fusion
  283.3 0.0 all-reduce.5.cloned.1.call-update
  283.3 0.2 all-gather.9.cloned.1.call-start
  283.5 220.3 %all-gather.7.cloned.1.call-done = bf16[2,4096,1024]{2,1,0:T(8,128)(2,1)} async-done(((bf16[2,512,1024]{2,1,0:T(8,128)(2,1)}), bf16[2,4096,1024]{2,1,0:T(8,128)(2,1)}) %all-gather.7.cloned.1.call-update) | async-done | bytes 16777232 | tf_op jit(solution)/shard_map/all_gather | solution.py:22
  503.8 153.4 %all-reduce.3.cloned.1.call-done = bf16[2,512,4096]{2,1,0:T(8,128)(2,1)} async-done(((bf16[2,512,4096]{2,1,0:T(8,128)(2,1)}), bf16[2,512,4096]{2,1,0:T(8,128)(2,1)}) %all-reduce.3.cloned.1.call-update) | async-done | bytes 8388624 | tf_op jit(solution)/shard_map/psum | solution.py:21
  657.2 15.8 %convolution_convert_fusion.2 = bf16[2,512,1024]{2,1,0:T(8,128)(2,1)} fusion(bf16[2,512,4096]{2,1,0:T(8,128)(2,1)} %all-reduce.3.cloned.1.call-done, bf16[2,4096,1024]{2,1,0:T(8,128)(2,1)} %all-gather.7.cloned.1.call-done), kind=kOutput, calls=%fused_computation.6 | convolution fusion | flops 8590983168 | bytes 27262976 | tf_op jit(solution)/shard_map/bij,bjk->bik/dot_general | solution.py:8
  673.0 0.0 all-gather.9.cloned.1.call-update
  673.0 258.1 %all-reduce.5.cloned.1.call-done = bf16[1024,4096]{1,0:T(8,128)(2,1)} async-done(((bf16[1024,4096]{1,0:T(8,128)(2,1)}), bf16[1024,4096]{1,0:T(8,128)(2,1)}) %all-reduce.5.cloned.1.call-update) | async-done | bytes 8388624 | tf_op jit(solution)/shard_map/psum | solution.py:18
  931.1 59.4 %all-gather.9.cloned.1.call-done = bf16[2,512,4096]{2,1,0:T(8,128)(2,1)} async-done(((bf16[2,512,1024]{2,1,0:T(8,128)(2,1)}), bf16[2,512,4096]{2,1,0:T(8,128)(2,1)}) %all-gather.9.cloned.1.call-update) | async-done | bytes 8388624 | tf_op jit(solution)/shard_map/all_gather | solution.py:24
  990.5 0.0 copy-start.1
  990.5 16.6 %divide_convert_fusion = (bf16[2,512,1024]{2,1,0:T(8,128)(2,1)}, bf16[2,512,1024]{2,1,0:T(8,128)(2,1)}) fusion(f32[2,512,1024]{2,1,0:T(8,128)} %param.7, bf16[2,512,4096]{2,1,0:T(8,128)(2,1)} %all-gather.9.cloned.1.call-done, bf16[1024,4096]{1,0:T(8,128)(2,1)} %all-reduce.5.cloned.1.call-done), kind=kOutput, calls=%fused_computation.4 | convolution fusion | flops 8595177472 | bytes 25165824 | tf_op jit(solution)/shard_map/bik,qk->biq/dot_general | solution.py:12
  1007.1 0.0 copy-done.1
Async XLA Ops:
  7.2 232.9 %copy-start = (bf16[2,1024,512]{2,1,0:T(8,128)(2,1)S(1)}, bf16[2,1024,512]{2,1,0:T(8,128)(2,1)}, u32[]{:S(2)}) copy-start(bf16[2,1024,512]{2,1,0:T(8,128)(2,1)} %param.9) | copy-start | bytes 6291460
  7.2 232.9 %all-gather.5.cloned.1.call-start = ((), (), s32[]{:S(2)}) async-start(), calls=%async_computation | async-start | bytes 18874368 | tf_op jit(solution)/shard_map/all_gather | solution.py:19
  7.9 266.4 %all-gather.11.cloned.1.call-start = ((), (), s32[]{:S(2)}) async-start(), calls=%async_computation.4 | async-start | bytes 5242880 | tf_op jit(solution)/shard_map/all_gather | solution.py:16
  8.7 495.1 %all-gather.7.cloned.1.call-start = ((), (), s32[]{:S(2)}) async-start(), calls=%async_computation.2 | async-start | bytes 18874368 | tf_op jit(solution)/shard_map/all_gather | solution.py:22
  9.4 647.8 %all-reduce.3.cloned.1.call-start = ((), (), s32[]{:S(2)}) async-start(), calls=%async_computation.1 | async-start | bytes 16777216 | tf_op jit(solution)/shard_map/psum | solution.py:21
  257.2 17.2 %copy-start.2 = (bf16[512,1024]{1,0:T(8,128)(2,1)S(1)}, bf16[512,1024]{1,0:T(8,128)(2,1)}, u32[]{:S(2)}) copy-start(bf16[512,1024]{1,0:T(8,128)(2,1)} %param.11) | copy-start | bytes 3145732
  257.2 673.9 %all-reduce.5.cloned.1.call-start = ((), (), s32[]{:S(2)}) async-start(), calls=%async_computation.5 | async-start | bytes 16777216 | tf_op jit(solution)/shard_map/psum | solution.py:18
  283.3 707.2 %all-gather.9.cloned.1.call-start = ((), (), s32[]{:S(2)}) async-start(), calls=%async_computation.3 | async-start | bytes 10485760 | tf_op jit(solution)/shard_map/all_gather | solution.py:24
  990.5 16.6 %copy-start.1 = (bf16[2,1024,512]{2,1,0:T(8,128)(2,1)S(1)}, bf16[2,1024,512]{2,1,0:T(8,128)(2,1)}, u32[]{:S(2)}) copy-start(bf16[2,1024,512]{2,1,0:T(8,128)(2,1)} %param.9) | copy-start | bytes 6291460
Sparse Core Ops, SparseCore 0:
  10.0 230.0 all-gather.4
  241.6 32.6 all-gather.10
  276.5 227.2 all-gather.6
  506.1 151.0 all-reduce.2
  660.9 270.1 all-reduce.4
  933.1 57.3 all-gather.8
where the time goes:
time: 1010 us
  waiting for transfers between devices  941 us (93%)
  matrix products  58.4 us (6%)
  between operations  14.1 us (1%)
    psum x1, waiting for transfers between devices, local(): right_panel = lax.psum(right_terms.astype(jnp.bfloat16), 'row')  258 us
    all_gather x1, waiting for transfers between devices, local(): old_rows = lax.all_gather(left_old, 'row', axis=2, tiled=True)  231 us
    all_gather x1, waiting for transfers between devices, local(): lax.all_gather(moment, 'row', axis=1, tiled=True)  220 us
    psum x1, waiting for transfers between devices, local(): left_panel = lax.psum(left_terms.astype(jnp.bfloat16), 'col')  153 us
    all_gather x1, waiting for transfers between devices, local(): lax.all_gather(rotated, 'col', axis=2, tiled=True)  59.4 us
  transfers between devices with their start and end apart: 6, of which 6 were waited for; matrix products, arithmetic and copies ran while one was open for 4% of the time, Pallas kernels for 0%

commit v1 on v0

--- a/solution.py
+++ b/solution.py
@@ -16,7 +16,12 @@
     old_right_rows = lax.all_gather(right_old, "col", axis=1, tiled=True)
     right_terms = jnp.dot(right_new.T, old_right_rows, preferred_element_type=jnp.float32)
     right_panel = lax.psum(right_terms.astype(jnp.bfloat16), "row")
-    old_rows = lax.all_gather(left_old, "row", axis=2, tiled=True)
+    ring = [left_old]
+    for hop in range(7):
+        ring.append(lax.ppermute(ring[-1], "row", [(dev, (dev + 1) % 8) for dev in range(8)]))
+    old_rows = jnp.roll(
+        jnp.concatenate(ring[::-1], axis=2), (lax.axis_index("row") + 1) * ring[0].shape[2], axis=2
+    )
     left_terms = jnp.einsum("bwi,bwj->bij", left_new, old_rows, preferred_element_type=jnp.float32)
     left_panel = lax.psum(left_terms.astype(jnp.bfloat16), "col")
     summed = fold_stacked(left_panel, lax.all_gather(moment, "row", axis=1, tiled=True))

time: 1010 us -> 1130 us (1.12)
  waiting for transfers between devices: 941 us -> 1020 us
  local copies, waits for them, and re-layouts: 0.02 us -> 37.2 us
    ppermute x0 -> x7, waiting for transfers between devices: none -> 333 us  [local(): lax.ppermute(ring[-1], 'row', [(dev, (dev + 1) % 8) for dev in range(8)])]
    all_gather x1 -> x0, waiting for transfers between devices: 231 us -> none  [local(): old_rows = lax.all_gather(left_old, 'row', axis=2, tiled=True)]
    unnamed x6 -> x43, local copies, waits for them, and re-layouts: 0.02 us -> 35.7 us
    all_gather x1, waiting for transfers between devices: 17.1 us -> 0.02 us  [local(): old_right_rows = lax.all_gather(right_old, 'col', axis=1, tiled=True)]
    psum x1, waiting for transfers between devices: 153 us -> 138 us  [local(): left_panel = lax.psum(left_terms.astype(jnp.bfloat16), 'col')]
  transfers between devices with their start and end apart: 6 -> 12, of which waited for: 6 -> 11; matrix products, arithmetic and copies ran while one was open for 4% -> 6% of each run, Pallas kernels for 0% -> 0%
where the time goes in v1:
time: 1130 us
  waiting for transfers between devices  1020 us (90%)
  matrix products  56.5 us (5%)
  local copies, waits for them, and re-layouts  37.2 us (3%)
  between operations  13.9 us (1%)
    ppermute x7, waiting for transfers between devices, local(): lax.ppermute(ring[-1], 'row', [(dev, (dev + 1) % 8) for dev in range(8)])  333 us
    psum x1, waiting for transfers between devices, local(): right_panel = lax.psum(right_terms.astype(jnp.bfloat16), 'row')  256 us
    all_gather x1, waiting for transfers between devices, local(): lax.all_gather(moment, 'row', axis=1, tiled=True)  230 us
    psum x1, waiting for transfers between devices, local(): left_panel = lax.psum(left_terms.astype(jnp.bfloat16), 'col')  138 us
    all_gather x1, waiting for transfers between devices, local(): lax.all_gather(rotated, 'col', axis=2, tiled=True)  59.4 us
    unnamed x43, local copies, waits for them, and re-layouts  35.7 us
  transfers between devices with their start and end apart: 12, of which 11 were waited for; matrix products, arithmetic and copies ran while one was open for 6% of the time, Pallas kernels for 0%

profile of v1, /device:TPU:0, one launch (start us, length us, event | category | flops | bytes accessed | tf_op | source)
XLA Modules:
  0.0 1128.4 jit_solution(14424567994983089632)
XLA Ops:
  7.2 0.0 all-gather.8.cloned.1.call-start
  7.2 3.0 collective-permute-start
  10.3 48.9 %collective-permute-done = bf16[2,1024,512]{2,1,0:T(8,128)(2,1)S(1)} collective-permute-done((bf16[2,1024,512]{2,1,0:T(8,128)(2,1)}, bf16[2,1024,512]{2,1,0:T(8,128)(2,1)S(1)}, u32[]{:S(2)}, u32[]{:S(2)}) %collective-permute-start) | collective-permute-done | bytes 2097184 | tf_op jit(solution)/shard_map/ppermute | solution.py:21
  59.2 1.3 copy-done.3
  60.4 49.5 %collective-permute-done.1 = bf16[2,1024,512]{2,1,0:T(8,128)(2,1)S(1)} collective-permute-done((bf16[2,1024,512]{2,1,0:T(8,128)(2,1)S(1)}, bf16[2,1024,512]{2,1,0:T(8,128)(2,1)S(1)}, u32[]{:S(2)}, u32[]{:S(2)}) %collective-permute-start.1) | collective-permute-done | bytes 2097184 | tf_op jit(solution)/shard_map/ppermute | solution.py:21
  109.9 1.4 copy-done.5
  111.3 48.6 %collective-permute-done.2 = bf16[2,1024,512]{2,1,0:T(8,128)(2,1)S(1)} collective-permute-done((bf16[2,1024,512]{2,1,0:T(8,128)(2,1)S(1)}, bf16[2,1024,512]{2,1,0:T(8,128)(2,1)S(1)}, u32[]{:S(2)}, u32[]{:S(2)}) %collective-permute-start.2) | collective-permute-done | bytes 2097184 | tf_op jit(solution)/shard_map/ppermute | solution.py:21
  159.9 1.4 copy-done.7
  161.3 47.8 %collective-permute-done.3 = bf16[2,1024,512]{2,1,0:T(8,128)(2,1)S(1)} collective-permute-done((bf16[2,1024,512]{2,1,0:T(8,128)(2,1)S(1)}, bf16[2,1024,512]{2,1,0:T(8,128)(2,1)S(1)}, u32[]{:S(2)}, u32[]{:S(2)}) %collective-permute-start.3) | collective-permute-done | bytes 2097184 | tf_op jit(solution)/shard_map/ppermute | solution.py:21
  209.1 1.3 copy-done.9
  210.4 46.9 %collective-permute-done.4 = bf16[2,1024,512]{2,1,0:T(8,128)(2,1)S(1)} collective-permute-done((bf16[2,1024,512]{2,1,0:T(8,128)(2,1)S(1)}, bf16[2,1024,512]{2,1,0:T(8,128)(2,1)S(1)}, u32[]{:S(2)}, u32[]{:S(2)}) %collective-permute-start.4) | collective-permute-done | bytes 2097184 | tf_op jit(solution)/shard_map/ppermute | solution.py:21
  257.3 1.3 copy-done.11
  258.6 46.2 %collective-permute-done.5 = bf16[2,1024,512]{2,1,0:T(8,128)(2,1)} collective-permute-done((bf16[2,1024,512]{2,1,0:T(8,128)(2,1)S(1)}, bf16[2,1024,512]{2,1,0:T(8,128)(2,1)}, u32[]{:S(2)}, u32[]{:S(2)}) %collective-permute-start.5) | collective-permute-done | bytes 2097184 | tf_op jit(solution)/shard_map/ppermute | solution.py:21
  304.8 0.0 all-gather.8.cloned.1.call-update
  304.8 0.0 all-reduce.3.cloned.1.call-start
  304.9 45.4 %collective-permute-done.6 = bf16[2,1024,512]{2,1,0:T(8,128)(2,1)} collective-permute-done((bf16[2,1024,512]{2,1,0:T(8,128)(2,1)}, bf16[2,1024,512]{2,1,0:T(8,128)(2,1)}, u32[]{:S(2)}, u32[]{:S(2)}) %collective-permute-start.6) | collective-permute-done | bytes 2097184 | tf_op jit(solution)/shard_map/ppermute | solution.py:21
  350.3 3.1 constant_dynamic-update-slice_fusion.15
  353.4 3.2 constant_dynamic-update-slice_fusion.14
  356.7 1.5 constant_dynamic-update-slice_fusion.13
  358.2 1.5 constant_dynamic-update-slice_fusion.12
  359.7 1.5 constant_dynamic-update-slice_fusion.11
  361.2 1.5 constant_dynamic-update-slice_fusion.10
  362.7 1.5 constant_dynamic-update-slice_fusion.9
  364.1 1.5 constant_dynamic-update-slice_fusion.8
  365.7 3.0 constant_dynamic-update-slice_fusion.7
  368.7 3.0 constant_dynamic-update-slice_fusion.6
  371.7 1.4 constant_dynamic-update-slice_fusion.5
  373.1 1.5 constant_dynamic-update-slice_fusion.4
  374.6 1.5 constant_dynamic-update-slice_fusion.3
  376.1 1.4 constant_dynamic-update-slice_fusion.2
  377.5 1.5 constant_dynamic-update-slice_fusion.1
  379.0 1.5 constant_dynamic-update-slice_fusion
  380.5 14.5 %convert_bitcast_fusion = bf16[2,512,4096]{1,2,0:T(8,128)(2,1)} fusion(bf16[2,1024,512]{2,1,0:T(8,128)(2,1)S(1)} %copy-done, bf16[2,1024,8192]{2,1,0:T(8,128)(2,1)} %constant_dynamic-update-slice_fusion, s32[]{:T(128)S(6)} %select_n.14), kind=kOutput, calls=%fused_computation.4 | convolution fusion | flops 8594128896 | bytes 27262980 | tf_op jit(solution)/shard_map/bwi,bwj->bij/dot_general | solution.py:25
  395.0 0.0 all-reduce.3.cloned.1.call-update
  395.0 0.0 all-gather.4.cloned.1.call-start
  395.0 0.7 all-gather.4.cloned.1.call-update
  395.7 0.0 all-reduce.5.cloned.1.call-start
  395.8 0.0 all-gather.8.cloned.1.call-done
  395.8 0.4 copy-done.13
  396.2 9.5 convolution_convert_fusion
  405.7 0.0 all-reduce.5.cloned.1.call-update
  405.7 0.2 all-gather.6.cloned.1.call-start
  405.9 138.4 %all-reduce.3.cloned.1.call-done = bf16[2,512,4096]{1,2,0:T(8,128)(2,1)} async-done(((bf16[2,512,4096]{1,2,0:T(8,128)(2,1)}), bf16[2,512,4096]{1,2,0:T(8,128)(2,1)}) %all-reduce.3.cloned.1.call-update) | async-done | bytes 8388624 | tf_op jit(solution)/shard_map/psum | solution.py:26
  544.3 229.6 %all-gather.4.cloned.1.call-done = bf16[2,4096,1024]{2,1,0:T(8,128)(2,1)} async-done(((bf16[2,512,1024]{2,1,0:T(8,128)(2,1)}), bf16[2,4096,1024]{2,1,0:T(8,128)(2,1)}) %all-gather.4.cloned.1.call-update) | async-done | bytes 16777232 | tf_op jit(solution)/shard_map/all_gather | solution.py:27
  773.9 15.9 %convolution_convert_fusion.1 = bf16[2,512,1024]{2,1,0:T(8,128)(2,1)} fusion(bf16[2,512,4096]{1,2,0:T(8,128)(2,1)} %all-reduce.3.cloned.1.call-done, bf16[2,4096,1024]{2,1,0:T(8,128)(2,1)} %all-gather.4.cloned.1.call-done), kind=kOutput, calls=%fused_computation.7 | convolution fusion | flops 8590983168 | bytes 27262976 | tf_op jit(solution)/shard_map/bij,bjk->bik/dot_general | solution.py:8
  789.8 256.0 %all-reduce.5.cloned.1.call-done = bf16[1024,4096]{1,0:T(8,128)(2,1)} async-done(((bf16[1024,4096]{1,0:T(8,128)(2,1)}), bf16[1024,4096]{1,0:T(8,128)(2,1)}) %all-reduce.5.cloned.1.call-update) | async-done | bytes 8388624 | tf_op jit(solution)/shard_map/psum | solution.py:18
  1045.9 59.4 %all-gather.6.cloned.1.call-done = bf16[2,512,4096]{2,1,0:T(8,128)(2,1)} async-done(((bf16[2,512,1024]{2,1,0:T(8,128)(2,1)}), bf16[2,512,4096]{2,1,0:T(8,128)(2,1)}) %all-gather.6.cloned.1.call-update) | async-done | bytes 8388624 | tf_op jit(solution)/shard_map/all_gather | solution.py:29
  1105.2 16.6 %divide_convert_fusion = (bf16[2,512,1024]{2,1,0:T(8,128)(2,1)}, bf16[2,512,1024]{2,1,0:T(8,128)(2,1)}) fusion(f32[2,512,1024]{2,1,0:T(8,128)} %param.7, bf16[2,512,4096]{2,1,0:T(8,128)(2,1)} %all-gather.6.cloned.1.call-done, bf16[1024,4096]{1,0:T(8,128)(2,1)} %all-reduce.5.cloned.1.call-done), kind=kOutput, calls=%fused_computation.6 | convolution fusion | flops 8595177472 | bytes 25165824 | tf_op jit(solution)/shard_map/bik,qk->biq/dot_general | solution.py:12
  (29 shorter events, 0.1 us)
Async XLA Ops:
  7.2 373.3 %copy-start = (bf16[2,1024,512]{2,1,0:T(8,128)(2,1)S(1)}, bf16[2,1024,512]{2,1,0:T(8,128)(2,1)}, u32[]{:S(2)}) copy-start(bf16[2,1024,512]{2,1,0:T(8,128)(2,1)} %param.9) | copy-start | bytes 6291460
  7.2 388.6 %all-gather.8.cloned.1.call-start = ((), (), s32[]{:S(2)}) async-start(), calls=%async_computation.3 | async-start | bytes 5242880 | tf_op jit(solution)/shard_map/all_gather | solution.py:16
  7.2 51.9 %collective-permute-start = (bf16[2,1024,512]{2,1,0:T(8,128)(2,1)}, bf16[2,1024,512]{2,1,0:T(8,128)(2,1)S(1)}, u32[]{:S(2)}, u32[]{:S(2)}) collective-permute-start(bf16[2,1024,512]{2,1,0:T(8,128)(2,1)} %param.8), channel_id=1, source_target_pairs={{0,4},{4,8},{8,12},{12,16},{16,20},{20,24},{24,28},{28,0},{1,5},{5... | collective-permute-start | bytes 6291464 | tf_op jit(solution)/shard_map/ppermute | solution.py:21
  59.2 1.3 copy-start.3
  60.4 49.5 %collective-permute-start.1 = (bf16[2,1024,512]{2,1,0:T(8,128)(2,1)S(1)}, bf16[2,1024,512]{2,1,0:T(8,128)(2,1)S(1)}, u32[]{:S(2)}, u32[]{:S(2)}) collective-permute-start(bf16[2,1024,512]{2,1,0:T(8,128)(2,1)S(1)} %collective-permute-done), channel_id=1, source_target_pairs={{0,4},{4,8},{8,12},{12,16},{16,20},{20,24},{24,28},{28,0},{1,5},{5... | collective-permute-start | bytes 6291464 | tf_op jit(solution)/shard_map/ppermute | solution.py:21
  109.9 1.4 copy-start.5
  111.3 48.6 %collective-permute-start.2 = (bf16[2,1024,512]{2,1,0:T(8,128)(2,1)S(1)}, bf16[2,1024,512]{2,1,0:T(8,128)(2,1)S(1)}, u32[]{:S(2)}, u32[]{:S(2)}) collective-permute-start(bf16[2,1024,512]{2,1,0:T(8,128)(2,1)S(1)} %collective-permute-done.1), channel_id=1, source_target_pairs={{0,4},{4,8},{8,12},{12,16},{16,20},{20,24},{24,28},{28,0},{1,5},{5... | collective-permute-start | bytes 6291464 | tf_op jit(solution)/shard_map/ppermute | solution.py:21
  159.9 1.4 copy-start.7
  161.3 47.8 %collective-permute-start.3 = (bf16[2,1024,512]{2,1,0:T(8,128)(2,1)S(1)}, bf16[2,1024,512]{2,1,0:T(8,128)(2,1)S(1)}, u32[]{:S(2)}, u32[]{:S(2)}) collective-permute-start(bf16[2,1024,512]{2,1,0:T(8,128)(2,1)S(1)} %collective-permute-done.2), channel_id=1, source_target_pairs={{0,4},{4,8},{8,12},{12,16},{16,20},{20,24},{24,28},{28,0},{1,5},{5... | collective-permute-start | bytes 6291464 | tf_op jit(solution)/shard_map/ppermute | solution.py:21
  209.1 1.3 copy-start.9
  210.4 46.9 %collective-permute-start.4 = (bf16[2,1024,512]{2,1,0:T(8,128)(2,1)S(1)}, bf16[2,1024,512]{2,1,0:T(8,128)(2,1)S(1)}, u32[]{:S(2)}, u32[]{:S(2)}) collective-permute-start(bf16[2,1024,512]{2,1,0:T(8,128)(2,1)S(1)} %collective-permute-done.3), channel_id=1, source_target_pairs={{0,4},{4,8},{8,12},{12,16},{16,20},{20,24},{24,28},{28,0},{1,5},{5... | collective-permute-start | bytes 6291464 | tf_op jit(solution)/shard_map/ppermute | solution.py:21
  257.3 1.3 copy-start.11
  258.6 46.2 %collective-permute-start.5 = (bf16[2,1024,512]{2,1,0:T(8,128)(2,1)S(1)}, bf16[2,1024,512]{2,1,0:T(8,128)(2,1)}, u32[]{:S(2)}, u32[]{:S(2)}) collective-permute-start(bf16[2,1024,512]{2,1,0:T(8,128)(2,1)S(1)} %collective-permute-done.4), channel_id=1, source_target_pairs={{0,4},{4,8},{8,12},{12,16},{16,20},{20,24},{24,28},{28,0},{1,5},{5... | collective-permute-start | bytes 6291464 | tf_op jit(solution)/shard_map/ppermute | solution.py:21
  304.8 45.5 %collective-permute-start.6 = (bf16[2,1024,512]{2,1,0:T(8,128)(2,1)}, bf16[2,1024,512]{2,1,0:T(8,128)(2,1)}, u32[]{:S(2)}, u32[]{:S(2)}) collective-permute-start(bf16[2,1024,512]{2,1,0:T(8,128)(2,1)} %collective-permute-done.5), channel_id=1, source_target_pairs={{0,4},{4,8},{8,12},{12,16},{16,20},{20,24},{24,28},{28,0},{1,5},{5... | collective-permute-start | bytes 6291464 | tf_op jit(solution)/shard_map/ppermute | solution.py:21
  304.8 239.5 %all-reduce.3.cloned.1.call-start = ((), (), s32[]{:S(2)}) async-start(), calls=%async_computation | async-start | bytes 16777216 | tf_op jit(solution)/shard_map/psum | solution.py:26
  304.9 51.8 %copy-start.12 = (bf16[2,1024,512]{2,1,0:T(8,128)(2,1)S(1)}, bf16[2,1024,512]{2,1,0:T(8,128)(2,1)}, u32[]{:S(2)}) copy-start(bf16[2,1024,512]{2,1,0:T(8,128)(2,1)} %copy-done.11) | copy-start | bytes 6291460
  304.9 53.2 %copy-start.10 = (bf16[2,1024,512]{2,1,0:T(8,128)(2,1)S(1)}, bf16[2,1024,512]{2,1,0:T(8,128)(2,1)}, u32[]{:S(2)}) copy-start(bf16[2,1024,512]{2,1,0:T(8,128)(2,1)} %copy-done.9) | copy-start | bytes 6291460
  304.9 54.8 %copy-start.8 = (bf16[2,1024,512]{2,1,0:T(8,128)(2,1)S(1)}, bf16[2,1024,512]{2,1,0:T(8,128)(2,1)}, u32[]{:S(2)}) copy-start(bf16[2,1024,512]{2,1,0:T(8,128)(2,1)} %copy-done.7) | copy-start | bytes 6291460
  353.4 7.7 copy-start.6
  356.7 6.0 copy-start.4
  358.2 6.0 copy-start.2
  395.0 1.2 copy-start.13
  395.0 378.9 %all-gather.4.cloned.1.call-start = ((), (), s32[]{:S(2)}) async-start(), calls=%async_computation.1 | async-start | bytes 18874368 | tf_op jit(solution)/shard_map/all_gather | solution.py:27
  395.7 650.1 %all-reduce.5.cloned.1.call-start = ((), (), s32[]{:S(2)}) async-start(), calls=%async_computation.4 | async-start | bytes 16777216 | tf_op jit(solution)/shard_map/psum | solution.py:18
  405.7 699.6 %all-gather.6.cloned.1.call-start = ((), (), s32[]{:S(2)}) async-start(), calls=%async_computation.2 | async-start | bytes 10485760 | tf_op jit(solution)/shard_map/all_gather | solution.py:29
  1105.2 16.6 %copy-start.1 = (bf16[2,1024,512]{2,1,0:T(8,128)(2,1)S(1)}, bf16[2,1024,512]{2,1,0:T(8,128)(2,1)}, u32[]{:S(2)}) copy-start(bf16[2,1024,512]{2,1,0:T(8,128)(2,1)} %param.9) | copy-start | bytes 6291460
Sparse Core Ops, SparseCore 0:
  305.0 35.0 all-gather.7
  395.1 149.1 all-reduce.2
  546.5 227.3 all-gather.3
  777.7 268.1 all-reduce.4
  1047.8 57.3 all-gather.5
